TPU v7x, 32 devices: a whole 2x2x4 slice. The times are simulated.
32 devices in a mesh: date: 16 (over z, y, x), pix: 2 (over core).
Axes of the slice: x: 2, y: 2, z: 4, core: 2. Of those that a mesh axis runs over, the one named last changes fastest.
Arguments:
- reflect: bfloat16 [64, 6, 16384], P('date', None, 'pix'), may hold values from -8 to 8
- cloud_free: int32 [64, 16384], P('date', 'pix'), may hold values from 0 to 1, as said below
- days: int32 [64], P('date'), may hold values from 1 to 2079, as said below
Outputs:
- median: float32 [6, 16384], P(None, 'pix')
- slope: float32 [6, 16384], P(None, 'pix')
Inputs may be any that keep to these rules, and one draw needn't show every extreme that they name: `cloud_free`: every pixel is clear on at least one of the first 32 dates and on at least one of the others; clear shares differ between tiles. `days`: strictly increasing.
All inputs are finite; a program needn't handle non-finite values.
Results may differ from a plain program's by a relative error of at most 0.0003.
Values may be sent and summed in bfloat16 or wider, within the bound.
A program may use at most 64 MiB of HBM per device.

v0:
```python
import jax
import jax.numpy as jnp
from jax import lax
from jax.sharding import PartitionSpec as P

ridge = 1.0
sentinel = 100.0


def count_ranks(carry, own, piece):

    def step(i, state):
        less, equal, count = state
        other = lax.dynamic_index_in_dim(piece, i, 0, keepdims=True).astype(jnp.float32)
        less = less + (other < own).astype(jnp.float32)
        equal = equal + (other == own).astype(jnp.float32)
        count = count + (other[0, 0] < 50.0).astype(jnp.float32)
        return (less, equal, count)

    return lax.fori_loop(0, piece.shape[0], step, carry)


def select_sums(values, valid, less, equal, count):
    lower = jnp.floor((count - 1.0) / 2.0)
    upper = jnp.floor(count / 2.0)
    low_pick = valid[:, None, :] * ((less <= lower) & (lower < less + equal)).astype(jnp.float32)
    high_pick = valid[:, None, :] * ((less <= upper) & (upper < less + equal)).astype(jnp.float32)
    return (
        jnp.sum(low_pick * values, 0),
        jnp.sum(low_pick, 0),
        jnp.sum(high_pick * values, 0),
        jnp.sum(high_pick, 0),
    )


def finish_median(low_num, low_den, high_num, high_den):
    return 0.5 * (low_num / jnp.maximum(low_den, 1.0) + high_num / jnp.maximum(high_den, 1.0))


def column_median(moved):
    column = moved.astype(jnp.float32)
    column_valid = (column[:, 0, :] < 50.0).astype(jnp.float32)
    zeros = jnp.zeros(column.shape, jnp.float32)
    start_carry = (zeros, zeros, jnp.zeros((column.shape[2],), jnp.float32))
    less, equal, count = count_ranks(start_carry, column, moved)
    low_num, low_den, high_num, high_den = select_sums(column, column_valid, less, equal, count)
    return (column, column_valid, finish_median(low_num, low_den, high_num, high_den))


def fit_slope(s_zero, s_one, s_two, s_y, s_ty):
    first = s_zero + ridge
    determinant = first * (s_two + ridge) - s_one * s_one
    return (first[None, :] * s_ty - s_one[None, :] * s_y) / determinant[None, :]


def local(reflect, cloud_free, days):
    values = reflect.astype(jnp.float32)
    valid = cloud_free.astype(jnp.float32)
    years = days.astype(jnp.float32) / 365.0
    csum = jnp.sum(values * valid[:, None, :], 2)
    cnt = jnp.sum(valid, 1)
    csum, cnt = lax.psum((csum, cnt), "pix")
    scene_mean = csum / jnp.maximum(cnt, 1.0)[:, None]
    marked = jnp.where(valid[:, None, :] > 0, values, sentinel).astype(jnp.bfloat16)
    shifted = values - scene_mean[:, :, None]
    weighted = valid[:, None, :] * shifted
    s_zero = jnp.sum(valid, 0)
    s_one = jnp.sum(years[:, None] * valid, 0)
    s_two = jnp.sum((years * years)[:, None] * valid, 0)
    s_y = jnp.sum(weighted, 0)
    s_ty = jnp.sum(years[:, None, None] * weighted, 0)
    moved = lax.all_to_all(marked, "date", split_axis=2, concat_axis=0, tiled=True)
    column, column_valid, part_median = column_median(moved)
    median = lax.all_gather(part_median, "date", axis=1, tiled=True)
    s_y, s_ty, s_zero, s_one, s_two = lax.psum((s_y, s_ty, s_zero, s_one, s_two), "date")
    slope = fit_slope(s_zero, s_one, s_two, s_y, s_ty)
    return (median, slope)


def solution(mesh):
    placed = (P("date", None, "pix"), P("date", "pix"), P("date"))
    return jax.shard_map(
        local,
        mesh=mesh,
        in_specs=placed,
        out_specs=(P(None, "pix"), P(None, "pix")),
        check_vma=False,
    )
```

profile of v0, /device:TPU:0, one launch (start us, length us, event | category | flops | bytes accessed | tf_op | source)
XLA Modules:
  0.0 414.7 jit_solution(17819752993265104546)
XLA Ops:
  7.9 1.8 convert_reduce_fusion.1
  9.7 0.9 convert_element_type.50
  10.7 1.0 broadcast_compare_fusion
  11.6 1.3 fusion.4
  12.9 2.6 all-reduce.2
  15.6 3.0 fusion.8
  18.6 8.5 %copy.37 = bf16[4,6,8192]{1,0,2:T(4,128)(2,1)} copy(bf16[4,6,8192]{2,0,1:T(4,128)(2,1)S(1)} %get-tuple-element.172) | data formatting | bytes 786432 | tf_op jit(solution)/shard_map/convert_element_type | solution.py:64
  27.2 14.3 %reshape.24 = bf16[16,2,6144]{2,1,0:T(2,128)(2,1)} reshape(bf16[8192,4,6]{2,1,0:T(4,128)(2,1)} %bitcast.17) | data formatting | bytes 786432
  41.5 8.2 %all-to-all-start = ((bf16[16,2,6144]{2,1,0:T(2,128)(2,1)}), bf16[16,2,6144]{2,1,0:T(2,128)(2,1)S(1)}, u32[]{:S(2)}, u32[]{:S(2)}) async-start(bf16[16,2,6144]{2,1,0:T(2,128)(2,1)} %reshape.24), calls=%async_computation | async-start | bytes 786432 | tf_op jit(solution)/shard_map/all_to_all | solution.py:72
  49.7 72.8 %all-reduce.6.cloned.1.call-done = (f32[8192]{0:T(1024)}, f32[8192]{0:T(1024)}, f32[8192]{0:T(1024)}) async-done(((f32[8192]{0:T(1024)}, f32[8192]{0:T(1024)}, f32[8192]{0:T(1024)}), (f32[8192]{0:T(1024)}, f32[8192]{0:T(1024)}, f32[8192]{0:T(1024)})) %all-reduce.6.cloned.1.call-update) | async-done | bytes 98320 | tf_op jit(solution)/shard_map/psum | solution.py:75
  122.5 0.8 broadcast_add_fusion
  123.4 114.3 %all-reduce.8.cloned.1.call-done = (f32[6,8192]{1,0:T(8,128)}, f32[6,8192]{1,0:T(8,128)}) async-done(((f32[6,8192]{1,0:T(8,128)}, f32[6,8192]{1,0:T(8,128)}), (f32[6,8192]{1,0:T(8,128)}, f32[6,8192]{1,0:T(8,128)})) %all-reduce.8.cloned.1.call-update) | async-done | bytes 393232 | tf_op jit(solution)/shard_map/psum | solution.py:75
  237.7 1.8 subtract_divide_fusion
  239.5 20.0 %reshape.25 = bf16[8192,4,6]{2,1,0:T(4,128)(2,1)} reshape(bf16[16,2,6144]{2,1,0:T(2,128)(2,1)S(1)} %all-to-all-done) | data formatting | bytes 786432
  259.5 12.9 %copy.38 = bf16[16,4,6,512]{3,2,1,0:T(8,128)(2,1)} copy(bf16[16,4,6,512]{2,1,3,0:T(4,128)(2,1)} %bitcast.18) | data formatting | bytes 786432 | tf_op jit(solution)/shard_map/all_to_all | solution.py:72
  272.3 1.2 bitcast_convert_fusion
  273.7 91.0 %while.18 = (s32[]{:T(128)}, f32[64,6,512]{2,1,0:T(8,128)S(1)}, f32[64,6,512]{2,1,0:T(8,128)S(1)}, f32[512]{0:T(512)S(1)}, bf16[64,6,512]{2,1,0:T(8,128)(2,1)}, ...) while((s32[]{:T(128)}, f32[64,6,512]{2,1,0:T(8,128)S(1)}, f32[64,6,512]{2,1,0:T(8,128)S(1)}, ...), condition=%wide.region_1.0_spmd.clone, body=%wide.region_0.0_spmd.clone.sunk | while | flops 1577987 | bytes 3985508 | solution.py:20
  273.7 0.7 dynamic-slice_convert_fusion.2
  275.1 0.7 dynamic-slice_convert_fusion.2
  276.5 0.7 dynamic-slice_convert_fusion.2
  277.9 0.7 dynamic-slice_convert_fusion.2
  279.4 0.7 dynamic-slice_convert_fusion.2
  365.1 1.6 fusion.1
  366.8 40.4 %all_gather.3 = f32[6,8192]{1,0:T(8,128)S(1)} all-gather(f32[6,512]{1,0:T(8,128)S(1)} %add_multiply_fusion), channel_id=1, replica_groups=mesh['date'=16,'pix'=2] {'date'}, dimensions={1}, use_global_device_ids=true | all-gather | bytes 208896 | tf_op jit(solution)/shard_map/all_gather | solution.py:74
  (268 shorter events, 87.7 us)
Async XLA Ops:
  7.2 115.4 %all-reduce.6.cloned.1.call-start = ((), (), s32[]{:S(2)}) async-start(), calls=%async_computation.1 | async-start | bytes 196608 | tf_op jit(solution)/shard_map/psum | solution.py:75
  9.7 228.0 %all-reduce.8.cloned.1.call-start = ((), (), s32[]{:S(2)}) async-start(), calls=%async_computation.2 | async-start | bytes 1048576 | tf_op jit(solution)/shard_map/psum | solution.py:75
  41.5 198.0 %all-to-all-start = ((bf16[16,2,6144]{2,1,0:T(2,128)(2,1)}), bf16[16,2,6144]{2,1,0:T(2,128)(2,1)S(1)}, u32[]{:S(2)}, u32[]{:S(2)}) async-start(bf16[16,2,6144]{2,1,0:T(2,128)(2,1)} %reshape.24), calls=%async_computation | async-start | bytes 786432 | tf_op jit(solution)/shard_map/all_to_all | solution.py:72
Sparse Core Ops, SparseCore 0:
  13.8 108.7 all-reduce.5
  128.3 109.3 all-reduce.7
where the time goes:
time: 419 us; the launch traced here: 415 us
  waiting for transfers between devices  187 us (45%)
  other arithmetic  104 us (25%)
  local copies, waits for them, and re-layouts  56.4 us (13%)
  blocking collectives  43 us (10%)
  between operations  14.1 us (3%)
  starting transfers between devices  8.26 us (2%)
    psum x2, waiting for transfers between devices, local(): lax.psum((s_y, s_ty, s_zero, s_one, s_two), 'date')  187 us
    convert_element_type x64, other arithmetic, step(): lax.dynamic_index_in_dim(piece, i, 0, keepdims=True).astype(jnp.float32)  45.1 us
    add x64, other arithmetic, step(): equal = equal + (other == own).astype(jnp.float32)  42.9 us
    all_gather x1, blocking collectives, local(): median = lax.all_gather(part_median, 'date', axis=1, tiled=True)  40.4 us
    unnamed x4, local copies, waits for them, and re-layouts  35 us
    all_to_all x1, local copies, waits for them, and re-layouts, local(): lax.all_to_all(marked, 'date', split_axis=2, concat_axis=0, tiled=True)  12.9 us
    convert_element_type x1, local copies, waits for them, and re-layouts, local(): jnp.where(valid[:, None, :] > 0, values, sentinel).astype(jnp.bfloat16)  8.54 us
  transfers between devices with their start and end apart: 3, of which 2 were waited for; matrix products, arithmetic and copies ran while one was open for 8% of the time, Pallas kernels for 0%

commit v1 on v0

--- a/solution.py
+++ b/solution.py
@@ -71,7 +71,13 @@
     s_ty = jnp.sum(years[:, None, None] * weighted, 0)
     moved = lax.all_to_all(marked, "date", split_axis=2, concat_axis=0, tiled=True)
     column, column_valid, part_median = column_median(moved)
-    median = lax.all_gather(part_median, "date", axis=1, tiled=True)
+    count_2 = lax.axis_size("date")
+    block, blocks = (part_median, [part_median])
+    for _ in range(count_2 - 1):
+        block = lax.ppermute(block, "date", [(i_2, (i_2 + 1) % count_2) for i_2 in range(count_2)])
+        blocks.insert(0, block)
+    merged = jnp.concatenate(blocks, axis=1)
+    median = jnp.roll(merged, (lax.axis_index("date") + 1) * part_median.shape[1], axis=1)
     s_y, s_ty, s_zero, s_one, s_two = lax.psum((s_y, s_ty, s_zero, s_one, s_two), "date")
     slope = fit_slope(s_zero, s_one, s_two, s_y, s_ty)
     return (median, slope)

time: 419 us -> 312 us (0.74)
  waiting for transfers between devices: 187 us -> 120 us
  blocking collectives: 43 us -> 2.62 us
    psum x2, waiting for transfers between devices: 187 us -> 0.01 us  [local(): lax.psum((s_y, s_ty, s_zero, s_one, s_two), 'date')]
    ppermute x0 -> x15, waiting for transfers between devices: none -> 107 us  [local(): lax.ppermute(block, 'date', [(i_2, (i_2 + 1) % count_2) for i_2 in range(...]
    all_gather x1 -> x0, blocking collectives: 40.4 us -> none  [local(): median = lax.all_gather(part_median, 'date', axis=1, tiled=True)]
    all_to_all x1, waiting for transfers between devices: 0.01 us -> 11.4 us  [local(): lax.all_to_all(marked, 'date', split_axis=2, concat_axis=0, tiled=True)]
    unnamed x4 -> x34, local copies, waits for them, and re-layouts: 35 us -> 34.4 us
  transfers between devices with their start and end apart: 3 -> 18, of which waited for: 2 -> 16; matrix products, arithmetic and copies ran while one was open for 8% -> 42% of each run, Pallas kernels for 0% -> 0%
where the time goes in v1:
time: 312 us; the launch traced here: 308 us
  waiting for transfers between devices  120 us (38%)
  other arithmetic  104 us (33%)
  local copies, waits for them, and re-layouts  56.5 us (18%)
  between operations  14.4 us (5%)
  starting transfers between devices  8.91 us (3%)
    ppermute x15, waiting for transfers between devices, local(): lax.ppermute(block, 'date', [(i_2, (i_2 + 1) % count_2) for i_2 in range(...  107 us
    convert_element_type x64, other arithmetic, step(): lax.dynamic_index_in_dim(piece, i, 0, keepdims=True).astype(jnp.float32)  45.1 us
    add x64, other arithmetic, step(): equal = equal + (other == own).astype(jnp.float32)  42.9 us
    unnamed x34, local copies, waits for them, and re-layouts  34.4 us
    all_to_all x1, local copies, waits for them, and re-layouts, local(): lax.all_to_all(marked, 'date', split_axis=2, concat_axis=0, tiled=True)  12.9 us
    all_to_all x1, waiting for transfers between devices, local(): lax.all_to_all(marked, 'date', split_axis=2, concat_axis=0, tiled=True)  11.4 us
    convert_element_type x1, local copies, waits for them, and re-layouts, local(): jnp.where(valid[:, None, :] > 0, values, sentinel).astype(jnp.bfloat16)  8.5 us
    all_to_all x1, starting transfers between devices, local(): lax.all_to_all(marked, 'date', split_axis=2, concat_axis=0, tiled=True)  8.18 us
  transfers between devices with their start and end apart: 18, of which 16 were waited for; matrix products, arithmetic and copies ran while one was open for 42% of the time, Pallas kernels for 0%

profile of v1, /device:TPU:0, one launch (start us, length us, event | category | flops | bytes accessed | tf_op | source)
XLA Modules:
  0.0 308.0 jit_solution(6323147509458287741)
XLA Ops:
  12.8 2.6 all-reduce.2
  15.5 3.0 fusion.8
  18.5 8.5 %copy.37 = bf16[4,6,8192]{1,0,2:T(4,128)(2,1)} copy(bf16[4,6,8192]{2,0,1:T(4,128)(2,1)S(1)} %get-tuple-element.172) | data formatting | bytes 786432 | tf_op jit(solution)/shard_map/convert_element_type | solution.py:64
  27.0 14.3 %reshape.24 = bf16[16,2,6144]{2,1,0:T(2,128)(2,1)} reshape(bf16[8192,4,6]{2,1,0:T(4,128)(2,1)} %bitcast.17) | data formatting | bytes 786432
  41.3 8.2 %all-to-all-start = ((bf16[16,2,6144]{2,1,0:T(2,128)(2,1)}), bf16[16,2,6144]{2,1,0:T(2,128)(2,1)S(1)}, u32[]{:S(2)}, u32[]{:S(2)}) async-start(bf16[16,2,6144]{2,1,0:T(2,128)(2,1)} %reshape.24), calls=%async_computation | async-start | bytes 786432 | tf_op jit(solution)/shard_map/all_to_all | solution.py:72
  51.0 11.4 %all-to-all-done = bf16[16,2,6144]{2,1,0:T(2,128)(2,1)S(1)} async-done(((bf16[16,2,6144]{2,1,0:T(2,128)(2,1)}), bf16[16,2,6144]{2,1,0:T(2,128)(2,1)S(1)}, u32[]{:S(2)}, u32[]{:S(2)}) %all-to-all-start) | async-done | bytes 393248 | tf_op jit(solution)/shard_map/all_to_all | solution.py:72
  62.4 20.0 %reshape.25 = bf16[8192,4,6]{2,1,0:T(4,128)(2,1)} reshape(bf16[16,2,6144]{2,1,0:T(2,128)(2,1)S(1)} %all-to-all-done) | data formatting | bytes 786432
  82.4 12.9 %copy.38 = bf16[16,4,6,512]{3,2,1,0:T(8,128)(2,1)} copy(bf16[16,4,6,512]{2,1,3,0:T(4,128)(2,1)} %bitcast.18) | data formatting | bytes 786432 | tf_op jit(solution)/shard_map/all_to_all | solution.py:72
  96.6 91.0 %while.18 = (s32[]{:T(128)}, f32[64,6,512]{2,1,0:T(8,128)S(1)}, f32[64,6,512]{2,1,0:T(8,128)S(1)}, f32[512]{0:T(512)S(1)}, bf16[64,6,512]{2,1,0:T(8,128)(2,1)}, ...) while((s32[]{:T(128)}, f32[64,6,512]{2,1,0:T(8,128)S(1)}, f32[64,6,512]{2,1,0:T(8,128)S(1)}, ...), condition=%wide.region_1.0_spmd.clone, body=%wide.region_0.0_spmd.clone.sunk | while | flops 1577987 | bytes 3985508 | solution.py:20
  190.3 6.8 %collective-permute-done = f32[6,512]{1,0:T(8,128)S(1)} collective-permute-done((f32[6,512]{1,0:T(8,128)S(1)}, f32[6,512]{1,0:T(8,128)S(1)}, u32[]{:S(2)}, u32[]{:S(2)}) %collective-permute-start) | collective-permute-done | bytes 12320 | tf_op jit(solution)/shard_map/ppermute | solution.py:77
  197.1 7.3 %collective-permute-done.1 = f32[6,512]{1,0:T(8,128)S(1)} collective-permute-done((f32[6,512]{1,0:T(8,128)S(1)}, f32[6,512]{1,0:T(8,128)S(1)}, u32[]{:S(2)}, u32[]{:S(2)}) %collective-permute-start.1) | collective-permute-done | bytes 12320 | tf_op jit(solution)/shard_map/ppermute | solution.py:77
  204.5 7.4 %collective-permute-done.2 = f32[6,512]{1,0:T(8,128)S(1)} collective-permute-done((f32[6,512]{1,0:T(8,128)S(1)}, f32[6,512]{1,0:T(8,128)S(1)}, u32[]{:S(2)}, u32[]{:S(2)}) %collective-permute-start.2) | collective-permute-done | bytes 12320 | tf_op jit(solution)/shard_map/ppermute | solution.py:77
  211.8 7.3 %collective-permute-done.3 = f32[6,512]{1,0:T(8,128)S(1)} collective-permute-done((f32[6,512]{1,0:T(8,128)S(1)}, f32[6,512]{1,0:T(8,128)S(1)}, u32[]{:S(2)}, u32[]{:S(2)}) %collective-permute-start.3) | collective-permute-done | bytes 12320 | tf_op jit(solution)/shard_map/ppermute | solution.py:77
  219.2 7.3 %collective-permute-done.4 = f32[6,512]{1,0:T(8,128)S(1)} collective-permute-done((f32[6,512]{1,0:T(8,128)S(1)}, f32[6,512]{1,0:T(8,128)S(1)}, u32[]{:S(2)}, u32[]{:S(2)}) %collective-permute-start.4) | collective-permute-done | bytes 12320 | tf_op jit(solution)/shard_map/ppermute | solution.py:77
  226.5 7.4 %collective-permute-done.5 = f32[6,512]{1,0:T(8,128)S(1)} collective-permute-done((f32[6,512]{1,0:T(8,128)S(1)}, f32[6,512]{1,0:T(8,128)S(1)}, u32[]{:S(2)}, u32[]{:S(2)}) %collective-permute-start.5) | collective-permute-done | bytes 12320 | tf_op jit(solution)/shard_map/ppermute | solution.py:77
  233.9 7.3 %collective-permute-done.6 = f32[6,512]{1,0:T(8,128)S(1)} collective-permute-done((f32[6,512]{1,0:T(8,128)S(1)}, f32[6,512]{1,0:T(8,128)S(1)}, u32[]{:S(2)}, u32[]{:S(2)}) %collective-permute-start.6) | collective-permute-done | bytes 12320 | tf_op jit(solution)/shard_map/ppermute | solution.py:77
  241.2 7.3 %collective-permute-done.7 = f32[6,512]{1,0:T(8,128)S(1)} collective-permute-done((f32[6,512]{1,0:T(8,128)S(1)}, f32[6,512]{1,0:T(8,128)S(1)}, u32[]{:S(2)}, u32[]{:S(2)}) %collective-permute-start.7) | collective-permute-done | bytes 12320 | tf_op jit(solution)/shard_map/ppermute | solution.py:77
  248.6 7.4 %collective-permute-done.8 = f32[6,512]{1,0:T(8,128)S(1)} collective-permute-done((f32[6,512]{1,0:T(8,128)S(1)}, f32[6,512]{1,0:T(8,128)S(1)}, u32[]{:S(2)}, u32[]{:S(2)}) %collective-permute-start.8) | collective-permute-done | bytes 12320 | tf_op jit(solution)/shard_map/ppermute | solution.py:77
  255.9 7.3 %collective-permute-done.9 = f32[6,512]{1,0:T(8,128)S(1)} collective-permute-done((f32[6,512]{1,0:T(8,128)S(1)}, f32[6,512]{1,0:T(8,128)S(1)}, u32[]{:S(2)}, u32[]{:S(2)}) %collective-permute-start.9) | collective-permute-done | bytes 12320 | tf_op jit(solution)/shard_map/ppermute | solution.py:77
  263.3 7.4 %collective-permute-done.10 = f32[6,512]{1,0:T(8,128)S(1)} collective-permute-done((f32[6,512]{1,0:T(8,128)S(1)}, f32[6,512]{1,0:T(8,128)S(1)}, u32[]{:S(2)}, u32[]{:S(2)}) %collective-permute-start.10) | collective-permute-done | bytes 12320 | tf_op jit(solution)/shard_map/ppermute | solution.py:77
  270.7 7.3 %collective-permute-done.11 = f32[6,512]{1,0:T(8,128)S(1)} collective-permute-done((f32[6,512]{1,0:T(8,128)S(1)}, f32[6,512]{1,0:T(8,128)S(1)}, u32[]{:S(2)}, u32[]{:S(2)}) %collective-permute-start.11) | collective-permute-done | bytes 12320 | tf_op jit(solution)/shard_map/ppermute | solution.py:77
  278.0 7.3 %collective-permute-done.12 = f32[6,512]{1,0:T(8,128)S(1)} collective-permute-done((f32[6,512]{1,0:T(8,128)S(1)}, f32[6,512]{1,0:T(8,128)S(1)}, u32[]{:S(2)}, u32[]{:S(2)}) %collective-permute-start.12) | collective-permute-done | bytes 12320 | tf_op jit(solution)/shard_map/ppermute | solution.py:77
  286.2 6.5 %collective-permute-done.13 = f32[6,512]{1,0:T(8,128)S(1)} collective-permute-done((f32[6,512]{1,0:T(8,128)S(1)}, f32[6,512]{1,0:T(8,128)S(1)}, u32[]{:S(2)}, u32[]{:S(2)}) %collective-permute-start.13) | collective-permute-done | bytes 12320 | tf_op jit(solution)/shard_map/ppermute | solution.py:77
  294.5 5.5 %collective-permute-done.14 = f32[6,512]{1,0:T(8,128)S(1)} collective-permute-done((f32[6,512]{1,0:T(8,128)S(1)}, f32[6,512]{1,0:T(8,128)S(1)}, u32[]{:S(2)}, u32[]{:S(2)}) %collective-permute-start.14) | collective-permute-done | bytes 12320 | tf_op jit(solution)/shard_map/ppermute | solution.py:77
  (329 shorter events, 103.8 us)
Async XLA Ops:
  41.3 21.1 %all-to-all-start = ((bf16[16,2,6144]{2,1,0:T(2,128)(2,1)}), bf16[16,2,6144]{2,1,0:T(2,128)(2,1)S(1)}, u32[]{:S(2)}, u32[]{:S(2)}) async-start(bf16[16,2,6144]{2,1,0:T(2,128)(2,1)} %reshape.24), calls=%async_computation | async-start | bytes 786432 | tf_op jit(solution)/shard_map/all_to_all | solution.py:72
  49.5 235.9 %all-reduce.6.cloned.1.call-start = ((), (), s32[]{:S(2)}) async-start(), calls=%async_computation.1 | async-start | bytes 196608 | tf_op jit(solution)/shard_map/psum | solution.py:81
  50.2 242.5 %all-reduce.8.cloned.1.call-start = ((), (), s32[]{:S(2)}) async-start(), calls=%async_computation.2 | async-start | bytes 1048576 | tf_op jit(solution)/shard_map/psum | solution.py:81
  189.7 7.4 %collective-permute-start = (f32[6,512]{1,0:T(8,128)S(1)}, f32[6,512]{1,0:T(8,128)S(1)}, u32[]{:S(2)}, u32[]{:S(2)}) collective-permute-start(f32[6,512]{1,0:T(8,128)S(1)} %add_multiply_fusion), channel_id=1, source_target_pairs={{0,2},{2,4},{4,6},{6,8},{8,10},{10,12},{12,14},{14,16},{16,18},{18... | collective-permute-start | bytes 36872 | tf_op jit(solution)/shard_map/ppermute | solution.py:77
  197.1 7.3 %collective-permute-start.1 = (f32[6,512]{1,0:T(8,128)S(1)}, f32[6,512]{1,0:T(8,128)S(1)}, u32[]{:S(2)}, u32[]{:S(2)}) collective-permute-start(f32[6,512]{1,0:T(8,128)S(1)} %collective-permute-done), channel_id=1, source_target_pairs={{0,2},{2,4},{4,6},{6,8},{8,10},{10,12},{12,14},{14,16},{16,18},{18... | collective-permute-start | bytes 36872 | tf_op jit(solution)/shard_map/ppermute | solution.py:77
  204.5 7.4 %collective-permute-start.2 = (f32[6,512]{1,0:T(8,128)S(1)}, f32[6,512]{1,0:T(8,128)S(1)}, u32[]{:S(2)}, u32[]{:S(2)}) collective-permute-start(f32[6,512]{1,0:T(8,128)S(1)} %collective-permute-done.1), channel_id=1, source_target_pairs={{0,2},{2,4},{4,6},{6,8},{8,10},{10,12},{12,14},{14,16},{16,18},{18... | collective-permute-start | bytes 36872 | tf_op jit(solution)/shard_map/ppermute | solution.py:77
  211.8 7.3 %collective-permute-start.3 = (f32[6,512]{1,0:T(8,128)S(1)}, f32[6,512]{1,0:T(8,128)S(1)}, u32[]{:S(2)}, u32[]{:S(2)}) collective-permute-start(f32[6,512]{1,0:T(8,128)S(1)} %collective-permute-done.2), channel_id=1, source_target_pairs={{0,2},{2,4},{4,6},{6,8},{8,10},{10,12},{12,14},{14,16},{16,18},{18... | collective-permute-start | bytes 36872 | tf_op jit(solution)/shard_map/ppermute | solution.py:77
  219.2 7.3 %collective-permute-start.4 = (f32[6,512]{1,0:T(8,128)S(1)}, f32[6,512]{1,0:T(8,128)S(1)}, u32[]{:S(2)}, u32[]{:S(2)}) collective-permute-start(f32[6,512]{1,0:T(8,128)S(1)} %collective-permute-done.3), channel_id=1, source_target_pairs={{0,2},{2,4},{4,6},{6,8},{8,10},{10,12},{12,14},{14,16},{16,18},{18... | collective-permute-start | bytes 36872 | tf_op jit(solution)/shard_map/ppermute | solution.py:77
  226.5 7.4 %collective-permute-start.5 = (f32[6,512]{1,0:T(8,128)S(1)}, f32[6,512]{1,0:T(8,128)S(1)}, u32[]{:S(2)}, u32[]{:S(2)}) collective-permute-start(f32[6,512]{1,0:T(8,128)S(1)} %collective-permute-done.4), channel_id=1, source_target_pairs={{0,2},{2,4},{4,6},{6,8},{8,10},{10,12},{12,14},{14,16},{16,18},{18... | collective-permute-start | bytes 36872 | tf_op jit(solution)/shard_map/ppermute | solution.py:77
  233.9 7.3 %collective-permute-start.6 = (f32[6,512]{1,0:T(8,128)S(1)}, f32[6,512]{1,0:T(8,128)S(1)}, u32[]{:S(2)}, u32[]{:S(2)}) collective-permute-start(f32[6,512]{1,0:T(8,128)S(1)} %collective-permute-done.5), channel_id=1, source_target_pairs={{0,2},{2,4},{4,6},{6,8},{8,10},{10,12},{12,14},{14,16},{16,18},{18... | collective-permute-start | bytes 36872 | tf_op jit(solution)/shard_map/ppermute | solution.py:77
  241.2 7.3 %collective-permute-start.7 = (f32[6,512]{1,0:T(8,128)S(1)}, f32[6,512]{1,0:T(8,128)S(1)}, u32[]{:S(2)}, u32[]{:S(2)}) collective-permute-start(f32[6,512]{1,0:T(8,128)S(1)} %collective-permute-done.6), channel_id=1, source_target_pairs={{0,2},{2,4},{4,6},{6,8},{8,10},{10,12},{12,14},{14,16},{16,18},{18... | collective-permute-start | bytes 36872 | tf_op jit(solution)/shard_map/ppermute | solution.py:77
  248.6 7.4 %collective-permute-start.8 = (f32[6,512]{1,0:T(8,128)S(1)}, f32[6,512]{1,0:T(8,128)S(1)}, u32[]{:S(2)}, u32[]{:S(2)}) collective-permute-start(f32[6,512]{1,0:T(8,128)S(1)} %collective-permute-done.7), channel_id=1, source_target_pairs={{0,2},{2,4},{4,6},{6,8},{8,10},{10,12},{12,14},{14,16},{16,18},{18... | collective-permute-start | bytes 36872 | tf_op jit(solution)/shard_map/ppermute | solution.py:77
  255.9 7.3 %collective-permute-start.9 = (f32[6,512]{1,0:T(8,128)S(1)}, f32[6,512]{1,0:T(8,128)S(1)}, u32[]{:S(2)}, u32[]{:S(2)}) collective-permute-start(f32[6,512]{1,0:T(8,128)S(1)} %collective-permute-done.8), channel_id=1, source_target_pairs={{0,2},{2,4},{4,6},{6,8},{8,10},{10,12},{12,14},{14,16},{16,18},{18... | collective-permute-start | bytes 36872 | tf_op jit(solution)/shard_map/ppermute | solution.py:77
  263.3 7.4 %collective-permute-start.10 = (f32[6,512]{1,0:T(8,128)S(1)}, f32[6,512]{1,0:T(8,128)S(1)}, u32[]{:S(2)}, u32[]{:S(2)}) collective-permute-start(f32[6,512]{1,0:T(8,128)S(1)} %collective-permute-done.9), channel_id=1, source_target_pairs={{0,2},{2,4},{4,6},{6,8},{8,10},{10,12},{12,14},{14,16},{16,18},{18... | collective-permute-start | bytes 36872 | tf_op jit(solution)/shard_map/ppermute | solution.py:77
  270.7 7.3 %collective-permute-start.11 = (f32[6,512]{1,0:T(8,128)S(1)}, f32[6,512]{1,0:T(8,128)S(1)}, u32[]{:S(2)}, u32[]{:S(2)}) collective-permute-start(f32[6,512]{1,0:T(8,128)S(1)} %collective-permute-done.10), channel_id=1, source_target_pairs={{0,2},{2,4},{4,6},{6,8},{8,10},{10,12},{12,14},{14,16},{16,18},{18... | collective-permute-start | bytes 36872 | tf_op jit(solution)/shard_map/ppermute | solution.py:77
  278.0 7.3 %collective-permute-start.12 = (f32[6,512]{1,0:T(8,128)S(1)}, f32[6,512]{1,0:T(8,128)S(1)}, u32[]{:S(2)}, u32[]{:S(2)}) collective-permute-start(f32[6,512]{1,0:T(8,128)S(1)} %collective-permute-done.11), channel_id=1, source_target_pairs={{0,2},{2,4},{4,6},{6,8},{8,10},{10,12},{12,14},{14,16},{16,18},{18... | collective-permute-start | bytes 36872 | tf_op jit(solution)/shard_map/ppermute | solution.py:77
  285.4 7.3 %collective-permute-start.13 = (f32[6,512]{1,0:T(8,128)S(1)}, f32[6,512]{1,0:T(8,128)S(1)}, u32[]{:S(2)}, u32[]{:S(2)}) collective-permute-start(f32[6,512]{1,0:T(8,128)S(1)} %collective-permute-done.12), channel_id=1, source_target_pairs={{0,2},{2,4},{4,6},{6,8},{8,10},{10,12},{12,14},{14,16},{16,18},{18... | collective-permute-start | bytes 36872 | tf_op jit(solution)/shard_map/ppermute | solution.py:77
  292.7 7.3 %collective-permute-start.14 = (f32[6,512]{1,0:T(8,128)S(1)}, f32[6,512]{1,0:T(8,128)S(1)}, u32[]{:S(2)}, u32[]{:S(2)}) collective-permute-start(f32[6,512]{1,0:T(8,128)S(1)} %collective-permute-done.13), channel_id=1, source_target_pairs={{0,2},{2,4},{4,6},{6,8},{8,10},{10,12},{12,14},{14,16},{16,18},{18... | collective-permute-start | bytes 36872 | tf_op jit(solution)/shard_map/ppermute | solution.py:77
Sparse Core Ops, SparseCore 0:
  56.1 107.3 all-reduce.5
  169.2 109.3 all-reduce.7
